TPU v7x, 32 devices: a whole 2x2x4 slice. The times are simulated.
32 devices in a mesh: grp: 4 (over x, core), lat: 8 (over z, y).
Axes of the slice: x: 2, y: 2, z: 4, core: 2. Of those that a mesh axis runs over, the one named last changes fastest.
Arguments:
- grid_state: bfloat16 [16, 192, 384, 128], P('grp', 'lat'), may hold values from -6 to 6
- noise_field: bfloat16 [16, 192, 384, 128], P('grp', 'lat'), may hold values from -6 to 6
- legendre: bfloat16 [192, 128, 128], P('lat'), may hold values from -0.4375 to 0.4375
- diffusion: float32 [128], replicated, may hold values from 0.1 to 10
- input_weight: bfloat16 [128, 256], replicated, may hold values from -0.5 to 0.5
- noise_weight: bfloat16 [128, 256], replicated, may hold values from -0.5 to 0.5
- input_bias: float32 [256], replicated, may hold values from -4 to 4
- middle_weight: bfloat16 [256, 256], replicated, may hold values from -0.375 to 0.375
- output_weight: bfloat16 [256, 128], replicated, may hold values from -0.375 to 0.375
Outputs:
- new_state: bfloat16 [16, 192, 384, 128], P('grp', 'lat')
- ens_mean: float32 [192, 384, 128], P('lat')
- ens_var: float32 [192, 384, 128], P('lat')
All inputs are finite; a program needn't handle non-finite values.
Results may differ from a plain program's by a relative error of at most 0.012.
Values may be sent and summed in bfloat16 or wider, within the bound.
A program may use at most 192 MiB of HBM per device.

v0:
```python
import math
import jax
import jax.numpy as jnp
from jax import lax
from jax.sharding import PartitionSpec as P


def wave_table(lon_count, wave_count):
    lon_ids = jnp.arange(lon_count, dtype=jnp.int32)[:, None]
    wave_ids = jnp.arange(wave_count, dtype=jnp.int32)[None, :]
    phase = (lon_ids * wave_ids % lon_count).astype(jnp.float32) * (2.0 * math.pi / lon_count)
    factor = math.sqrt(2.0 / lon_count)
    joined = jnp.concatenate([jnp.cos(phase), -jnp.sin(phase)], axis=1) * factor
    return joined.astype(jnp.bfloat16)


def damping_filter(diffusion, wave_count):
    degree = jnp.arange(wave_count, dtype=jnp.int32).astype(jnp.float32)
    ratio = degree * (degree + 1.0) / float((wave_count - 1) * wave_count)
    return 1.0 / (1.0 + diffusion[None, :] * (ratio * ratio)[:, None])


def per_device(
    grid_state,
    noise_field,
    legendre,
    diffusion,
    input_weight,
    noise_weight,
    input_bias,
    middle_weight,
    output_weight,
):
    members, lat_rows, lon_count, channels = grid_state.shape
    wave_count = legendre.shape[1]
    local_waves = wave_count // lax.axis_size("lat")
    transform = wave_table(lon_count, wave_count)
    fourier = jnp.einsum(
        "blxc,xk->blkc", grid_state, transform, preferred_element_type=jnp.float32
    ).astype(jnp.bfloat16)
    fourier = fourier.reshape(members, lat_rows, 2, wave_count, channels)
    basis_band = lax.all_to_all(legendre, "lat", split_axis=1, concat_axis=0, tiled=True)
    zonal_ids = lax.axis_index("lat") * local_waves + jnp.arange(local_waves, dtype=jnp.int32)
    total_ids = jnp.arange(wave_count, dtype=jnp.int32)
    triangle = (total_ids[None, :] >= zonal_ids[:, None]).astype(jnp.float32)
    damping = damping_filter(diffusion, wave_count)
    spectrum = jnp.einsum(
        "lmn,blrmc->brmnc",
        basis_band,
        lax.all_to_all(fourier, "lat", split_axis=3, concat_axis=1, tiled=True),
        preferred_element_type=jnp.float32,
    )
    spectrum = spectrum * triangle[None, None, :, :, None]
    filtered = (spectrum * damping[None, None, None, :, :]).astype(jnp.bfloat16)
    banded_grid = jnp.einsum(
        "lmn,brmnc->blrmc", basis_band, filtered, preferred_element_type=jnp.float32
    ).astype(jnp.bfloat16)
    grid_fourier = lax.all_to_all(banded_grid, "lat", split_axis=1, concat_axis=3, tiled=True)
    grid_fourier = grid_fourier.reshape(members, lat_rows, 2 * wave_count, channels)
    smoothed = jnp.einsum(
        "bljc,xj->blxc", grid_fourier, transform, preferred_element_type=jnp.float32
    )
    flat_fields = smoothed.reshape(-1, channels)
    smoothed_in = flat_fields.astype(jnp.bfloat16)
    pre_act = jnp.dot(smoothed_in, input_weight, preferred_element_type=jnp.float32)
    pre_act = pre_act + jnp.dot(
        noise_field.reshape(-1, noise_field.shape[3]),
        noise_weight,
        preferred_element_type=jnp.float32,
    )
    hidden_one = jax.nn.silu(pre_act + input_bias).astype(jnp.bfloat16)
    hidden_two = jax.nn.silu(
        jnp.dot(hidden_one, middle_weight, preferred_element_type=jnp.float32)
    ).astype(jnp.bfloat16)
    tendency = jnp.dot(hidden_two, output_weight, preferred_element_type=jnp.float32)
    new_state = (flat_fields + tendency).astype(jnp.bfloat16).reshape(grid_state.shape)
    member_values = new_state.astype(jnp.float32)
    ensemble = members * lax.axis_size("grp")
    summed = lax.psum(jnp.sum(member_values, axis=0).astype(jnp.bfloat16), "grp").astype(
        jnp.float32
    )
    ens_mean = summed / ensemble
    spread = lax.psum(
        jnp.sum(jnp.square(member_values - ens_mean), axis=0).astype(jnp.bfloat16), "grp"
    ).astype(jnp.float32)
    ens_var = spread / (ensemble - 1)
    return (new_state, ens_mean, ens_var)


def solution(mesh):
    in_specs = (
        P("grp", "lat", None, None),
        P("grp", "lat", None, None),
        P("lat", None, None),
        P(),
        P(),
        P(),
        P(),
        P(),
        P(),
    )
    out_specs = (P("grp", "lat", None, None), P("lat", None, None), P("lat", None, None))
    return jax.shard_map(
        per_device, mesh=mesh, in_specs=in_specs, out_specs=out_specs, check_vma=False
    )
```

profile of v0, /device:TPU:0, one launch (start us, length us, event | category | flops | bytes accessed | tf_op | source)
XLA Modules:
  0.0 592.4 jit_solution(8928592732857764437)
XLA Ops:
  7.2 2.6 copy.27
  9.7 7.3 %all-to-all-start.1 = ((bf16[24,128,128]{2,0,1:T(8,128)(2,1)}), bf16[24,128,128]{2,0,1:T(8,128)(2,1)S(1)}, u32[]{:S(2)}, u32[]{:S(2)}) async-start(bf16[24,128,128]{2,0,1:T(8,128)(2,1)} %copy.27), calls=%async_computation.1 | async-start | bytes 1572864 | tf_op jit(solution)/shard_map/all_to_all | solution.py:42
  17.9 7.4 %convolution_convert_fusion = bf16[256,4,24,128]{3,0,2,1:T(8,128)(2,1)S(1)} fusion(bf16[4,24,384,128]{3,2,1,0:T(8,128)(2,1)} %param.9, f32[384,128]{0,1:T(8,128)S(1)} %get-tuple-element.3, f32[384,128]{0,1:T(8,128)S(1)} %get-tuple-element.4), kind=kOutput, calls=%fused_computation.19 | convolution fusion | flops 2419359744 | bytes 16121856 | tf_op jit(solution)/shard_map/blxc,xk->blkc/dot_general | solution.py:38
  25.2 20.3 %copy.24 = bf16[4,24,2,128,128]{4,2,1,0,3:T(2,128)(2,1)} copy(bf16[4,24,2,128,128]{4,3,2,1,0:T(8,128)(2,1)S(1)} %bitcast.52) | data formatting | bytes 12582912 | tf_op jit(solution)/shard_map/reshape | solution.py:41
  45.6 6.1 %all-to-all-start = ((bf16[4,24,2,128,128]{4,2,1,0,3:T(2,128)(2,1)}), bf16[4,24,2,128,128]{4,2,1,0,3:T(2,128)(2,1)}, u32[]{:S(2)}, u32[]{:S(2)}) async-start(bf16[4,24,2,128,128]{4,2,1,0,3:T(2,128)(2,1)} %copy.24), calls=%async_computation | async-start | bytes 12582912 | tf_op jit(solution)/shard_map/all_to_all | solution.py:50
  52.5 136.8 %all-to-all-done = bf16[4,24,2,128,128]{4,2,1,0,3:T(2,128)(2,1)} async-done(((bf16[4,24,2,128,128]{4,2,1,0,3:T(2,128)(2,1)}), bf16[4,24,2,128,128]{4,2,1,0,3:T(2,128)(2,1)}, u32[]{:S(2)}, u32[]{:S(2)}) %all-to-all-start) | async-done | bytes 6291488 | tf_op jit(solution)/shard_map/all_to_all | solution.py:50
  189.4 10.1 %copy.25 = bf16[4,24,2,128,128]{4,3,2,1,0:T(8,128)(2,1)S(1)} copy(bf16[4,24,2,128,128]{4,2,1,0,3:T(2,128)(2,1)} %all-to-all-done) | data formatting | bytes 12582912 | tf_op jit(solution)/shard_map/all_to_all | solution.py:50
  199.4 4.4 copy.26
  203.8 8.5 %convert_bitcast_fusion = bf16[4,192,2,16,128]{4,1,2,0,3:T(8,128)(2,1)} fusion(bf16[192,16,128,1,1]{2,0,4,3,1:T(8,128)(2,1)S(1)} %bitcast.61, f32[128,128]{0,1:T(8,128)S(1)} %add_divide_fusion, f32[16,128]{1,0:T(8,128)S(1)} %fusion.27, bf16[4,192,2,16,128]{4,3,2,1,0:T(8,128)(2,1)} %bitcast.59), kind=kOutput, calls=%fused_computation.13 | convolution fusion | flops 1620049920 | bytes 13443072 | tf_op jit(solution)/shard_map/lmn,brmnc->blrmc/dot_general | solution.py:55
  212.3 9.5 %copy.31 = bf16[4,192,2,16,128]{4,2,0,3,1:T(2,128)(2,1)S(1)} copy(bf16[4,192,2,16,128]{4,1,2,0,3:T(8,128)(2,1)} %convert_bitcast_fusion) | data formatting | bytes 12582912 | tf_op jit(solution)/shard_map/convert_element_type | solution.py:57
  221.8 141.7 %all_to_all.51 = bf16[4,192,2,16,128]{4,2,0,3,1:T(2,128)(2,1)S(1)} all-to-all(bf16[4,192,2,16,128]{4,2,0,3,1:T(2,128)(2,1)S(1)} %copy.31), channel_id=1, replica_groups=mesh['grp'=4,'lat'=8] {'lat'}, dimensions={1} | all-to-all | bytes 12582912 | tf_op jit(solution)/shard_map/all_to_all | solution.py:58
  363.5 1.8 copy.32
  365.3 2.7 fusion.25
  368.0 6.4 %copy-done.2 = f32[384,4,24,128]{3,0,2,1:T(8,128)} copy-done((f32[384,4,24,128]{3,0,2,1:T(8,128)}, f32[384,4,24,128]{3,0,2,1:T(8,128)S(1)}, u32[]{:S(2)}) %copy-start.2) | copy-done | bytes 18874392
  374.5 4.3 bitcast_convert_fusion
  378.8 17.0 %fusion.36 = f32[36864,256]{1,0:T(8,128)} fusion(bf16[36864,128]{1,0:T(8,128)(2,1)} %bitcast_convert_fusion, bf16[128,256]{1,0:T(8,128)(2,1)S(1)} %copy-done.3), kind=kOutput, calls=%fused_computation.46 | convolution fusion | flops 2415919104 | bytes 47251456 | tf_op jit(solution)/shard_map/dot_general | solution.py:65
  395.7 27.9 %fusion.2 = f32[36864,256]{1,0:T(8,128)} fusion(bf16[256,256]{1,0:T(8,128)(2,1)S(1)} %copy-done, f32[36864,256]{1,0:T(8,128)} %fusion.36, bf16[36864,128]{1,0:T(8,128)(2,1)} %bitcast.62, bf16[128,256]{1,0:T(8,128)(2,1)S(1)} %copy-done.5, f32[256]{0:T(256)S(1)} %copy-done.7), kind=kOutput, calls=%fused_computation.8 | convolution fusion | flops 7313817600 | bytes 85132288 | tf_op jit(solution)/shard_map/dot_general | solution.py:73
  423.6 24.7 %fusion.1 = bf16[36864,128]{1,0:T(8,128)(2,1)} fusion(f32[36864,128]{1,0:T(8,128)} %bitcast.51, bf16[256,128]{1,0:T(8,128)(2,1)S(1)} %copy-done.6, f32[36864,256]{1,0:T(8,128)} %fusion.2), kind=kOutput, calls=%fused_computation.3 | convolution fusion | flops 2472542208 | bytes 66125824 | tf_op jit(solution)/shard_map/dot_general | solution.py:75
  448.3 7.6 %reduce_sum.21 = bf16[24,384,128]{2,1,0:T(8,128)(2,1)} reduce(bf16[4,24,384,128]{3,2,1,0:T(8,128)(2,1)} %bitcast.53, bf16[]{:T(256)} %constant.37.clone.1), dimensions={0}, to_apply=%region_0.1 | reduce | flops 3538944 | bytes 11796482 | tf_op jit(solution)/shard_map/reduce_sum | solution.py:79
  455.9 54.8 %all-reduce.3.cloned.1.call-done = bf16[24,384,128]{2,1,0:T(8,128)(2,1)} async-done(((bf16[24,384,128]{2,1,0:T(8,128)(2,1)}), bf16[24,384,128]{2,1,0:T(8,128)(2,1)}) %all-reduce.3.cloned.1.call-update) | async-done | bytes 2359312 | tf_op jit(solution)/shard_map/psum | solution.py:79
  510.7 4.4 convert_multiply_fusion.1
  515.2 9.8 %multiply_reduce_fusion = bf16[24,384,128]{2,1,0:T(8,128)(2,1)} fusion(bf16[4,24,384,128]{3,2,1,0:T(8,128)(2,1)} %bitcast.54, f32[24,384,128]{2,1,0:T(8,128)} %convert_multiply_fusion.1), kind=kLoop, calls=%fused_computation.7 | loop fusion | flops 17694720 | bytes 16515072 | tf_op jit(solution)/shard_map/reduce_sum | solution.py:84
  525.0 55.9 %all-reduce.5.cloned.1.call-done = bf16[24,384,128]{2,1,0:T(8,128)(2,1)} async-done(((bf16[24,384,128]{2,1,0:T(8,128)(2,1)}), bf16[24,384,128]{2,1,0:T(8,128)(2,1)}) %all-reduce.5.cloned.1.call-update) | async-done | bytes 2359312 | tf_op jit(solution)/shard_map/psum | solution.py:83
  580.8 4.4 convert_multiply_fusion
  (26 shorter events, 1.7 us)
Async XLA Ops:
  7.2 388.6 %copy-start = (bf16[256,256]{1,0:T(8,128)(2,1)S(1)}, bf16[256,256]{1,0:T(8,128)(2,1)}, u32[]{:S(2)}) copy-start(bf16[256,256]{1,0:T(8,128)(2,1)} %param.16) | copy-start | bytes 393220
  9.7 35.8 %all-to-all-start.1 = ((bf16[24,128,128]{2,0,1:T(8,128)(2,1)}), bf16[24,128,128]{2,0,1:T(8,128)(2,1)S(1)}, u32[]{:S(2)}, u32[]{:S(2)}) async-start(bf16[24,128,128]{2,0,1:T(8,128)(2,1)} %copy.27), calls=%async_computation.1 | async-start | bytes 1572864 | tf_op jit(solution)/shard_map/all_to_all | solution.py:42
  45.6 6.7 %copy-start.4 = (f32[128]{0:T(128)S(1)}, f32[128]{0:T(128)}, u32[]{:S(2)}) copy-start(f32[128]{0:T(128)} %param.12) | copy-start | bytes 1540
  45.6 143.8 %all-to-all-start = ((bf16[4,24,2,128,128]{4,2,1,0,3:T(2,128)(2,1)}), bf16[4,24,2,128,128]{4,2,1,0,3:T(2,128)(2,1)}, u32[]{:S(2)}, u32[]{:S(2)}) async-start(bf16[4,24,2,128,128]{4,2,1,0,3:T(2,128)(2,1)} %copy.24), calls=%async_computation | async-start | bytes 12582912 | tf_op jit(solution)/shard_map/all_to_all | solution.py:50
  51.7 459.0 %all-reduce.3.cloned.1.call-start = ((), (), s32[]{:S(2)}) async-start(), calls=%async_computation.3 | async-start | bytes 4718592 | tf_op jit(solution)/shard_map/psum | solution.py:79
  368.0 6.5 %copy-start.2 = (f32[384,4,24,128]{3,0,2,1:T(8,128)}, f32[384,4,24,128]{3,0,2,1:T(8,128)S(1)}, u32[]{:S(2)}) copy-start(f32[384,4,24,128]{3,0,2,1:T(8,128)S(1)} %fusion.25) | copy-start | bytes 56623108
  374.5 4.3 copy-start.3
  378.8 17.0 %copy-start.5 = (bf16[128,256]{1,0:T(8,128)(2,1)S(1)}, bf16[128,256]{1,0:T(8,128)(2,1)}, u32[]{:S(2)}) copy-start(bf16[128,256]{1,0:T(8,128)(2,1)} %param.14) | copy-start | bytes 196612
  378.8 17.0 %copy-start.7 = (f32[256]{0:T(256)S(1)}, f32[256]{0:T(256)}, u32[]{:S(2)}) copy-start(f32[256]{0:T(256)} %param.15) | copy-start | bytes 3076
  395.7 27.9 %copy-start.6 = (bf16[256,128]{1,0:T(8,128)(2,1)S(1)}, bf16[256,128]{1,0:T(8,128)(2,1)}, u32[]{:S(2)}) copy-start(bf16[256,128]{1,0:T(8,128)(2,1)} %param.17) | copy-start | bytes 196612
  455.9 125.0 %all-reduce.5.cloned.1.call-start = ((), (), s32[]{:S(2)}) async-start(), calls=%async_computation.4 | async-start | bytes 4718592 | tf_op jit(solution)/shard_map/psum | solution.py:83
  510.7 74.6 %copy-start.1 = (bf16[256,256]{1,0:T(8,128)(2,1)S(1)}, bf16[256,256]{1,0:T(8,128)(2,1)}, u32[]{:S(2)}) copy-start(bf16[256,256]{1,0:T(8,128)(2,1)} %param.16) | copy-start | bytes 393220
Sparse Core Ops, SparseCore 0:
  456.0 54.6 all-reduce.2
  525.1 55.7 all-reduce.4
where the time goes:
time: 597 us; the launch traced here: 592 us
  waiting for transfers between devices  248 us (42%)
  blocking collectives  142 us (24%)
  matrix products  88 us (15%)
  local copies, waits for them, and re-layouts  55.2 us (9%)
  other arithmetic  31.5 us (5%)
  between operations  14.4 us (2%)
  starting transfers between devices  14 us (2%)
    all_to_all x1, blocking collectives, per_device(): lax.all_to_all(banded_grid, 'lat', split_axis=1, concat_axis=3, tiled=True)  142 us
    all_to_all x1, waiting for transfers between devices, per_device(): lax.all_to_all(fourier, 'lat', split_axis=3, concat_axis=1, tiled=True)  137 us
    psum x1, waiting for transfers between devices, per_device(): lax.psum(jnp.sum(jnp.square(member_values - ens_mean), axis=0).astype(jnp...  55.9 us
    psum x1, waiting for transfers between devices, per_device(): lax.psum(jnp.sum(member_values, axis=0).astype(jnp.bfloat16), 'grp')  54.8 us
    dot_general x1, matrix products, per_device(): jnp.dot(hidden_one, middle_weight, preferred_element_type=jnp.float32)  27.9 us
    dot_general x1, matrix products, per_device(): jnp.dot(hidden_two, output_weight, preferred_element_type=jnp.float32)  24.7 us
    reshape x1, local copies, waits for them, and re-layouts, per_device(): fourier = fourier.reshape(members, lat_rows, 2, wave_count, channels)  20.3 us
    dot_general x1, matrix products, per_device(): jnp.dot(smoothed_in, input_weight, preferred_element_type=jnp.float32)  17 us
  transfers between devices with their start and end apart: 4, of which 3 were waited for; matrix products, arithmetic and copies ran while one was open for 5% of the time, Pallas kernels for 0%

commit v1 on v0

--- a/solution.py
+++ b/solution.py
@@ -3,6 +3,12 @@
 import jax.numpy as jnp
 from jax import lax
 from jax.sharding import PartitionSpec as P
+
+
+def stacked_exchange(value, name, split, join):
+    cells = jnp.split(value, lax.axis_size(name), axis=split)
+    arrived = lax.all_to_all(jnp.stack(cells), name, 0, 0)
+    return jnp.concatenate(arrived, axis=join)
 
 
 def wave_table(lon_count, wave_count):
@@ -47,7 +53,7 @@
     spectrum = jnp.einsum(
         "lmn,blrmc->brmnc",
         basis_band,
-        lax.all_to_all(fourier, "lat", split_axis=3, concat_axis=1, tiled=True),
+        stacked_exchange(fourier, "lat", 3, 1),
         preferred_element_type=jnp.float32,
     )
     spectrum = spectrum * triangle[None, None, :, :, None]

time: 597 us -> 575 us (0.963)
  local copies, waits for them, and re-layouts: 55.2 us -> 36.4 us
    reshape x1 -> x0, local copies, waits for them, and re-layouts: 20.3 us -> none  [per_device(): fourier = fourier.reshape(members, lat_rows, 2, wave_count, channels)]
    unnamed x17 -> x24, local copies, waits for them, and re-layouts: 9.04 us -> 16.6 us
    all_to_all x2 -> x1, local copies, waits for them, and re-layouts: 14.4 us -> 7.25 us  [stacked_exchange(): arrived = lax.all_to_all(jnp.stack(cells), name, 0, 0)]
  transfers between devices with their start and end apart: 4 -> 4, of which waited for: 3 -> 4; matrix products, arithmetic and copies ran while one was open for 5% -> 3% of each run, Pallas kernels for 0% -> 0%
where the time goes in v1:
time: 575 us; the launch traced here: 574 us
  waiting for transfers between devices  251 us (44%)
  blocking collectives  142 us (25%)
  matrix products  87.9 us (15%)
  local copies, waits for them, and re-layouts  36.4 us (6%)
  other arithmetic  31.5 us (5%)
  between operations  14.1 us (2%)
  starting transfers between devices  12.1 us (2%)
    all_to_all x1, blocking collectives, per_device(): lax.all_to_all(banded_grid, 'lat', split_axis=1, concat_axis=3, tiled=True)  142 us
    all_to_all x1, waiting for transfers between devices, stacked_exchange(): arrived = lax.all_to_all(jnp.stack(cells), name, 0, 0)  137 us
    psum x1, waiting for transfers between devices, per_device(): lax.psum(jnp.sum(jnp.square(member_values - ens_mean), axis=0).astype(jnp...  55.9 us
    psum x1, waiting for transfers between devices, per_device(): lax.psum(jnp.sum(member_values, axis=0).astype(jnp.bfloat16), 'grp')  54.8 us
    dot_general x1, matrix products, per_device(): jnp.dot(hidden_one, middle_weight, preferred_element_type=jnp.float32)  27.9 us
    dot_general x1, matrix products, per_device(): jnp.dot(hidden_two, output_weight, preferred_element_type=jnp.float32)  24.7 us
    dot_general x1, matrix products, per_device(): jnp.dot(smoothed_in, input_weight, preferred_element_type=jnp.float32)  17 us
    unnamed x24, local copies, waits for them, and re-layouts  16.6 us
  transfers between devices with their start and end apart: 4, of which 4 were waited for; matrix products, arithmetic and copies ran while one was open for 3% of the time, Pallas kernels for 0%

profile of v1, /device:TPU:0, one launch (start us, length us, event | category | flops | bytes accessed | tf_op | source)
XLA Modules:
  0.0 574.5 jit_solution(5132565784148475371)
XLA Ops:
  7.2 2.6 copy.26
  9.7 7.3 %all-to-all-start.1 = ((bf16[24,128,128]{2,0,1:T(8,128)(2,1)}), bf16[24,128,128]{2,0,1:T(8,128)(2,1)S(1)}, u32[]{:S(2)}, u32[]{:S(2)}) async-start(bf16[24,128,128]{2,0,1:T(8,128)(2,1)} %copy.26), calls=%async_computation.1 | async-start | bytes 1572864 | tf_op jit(solution)/shard_map/all_to_all | solution.py:48
  17.9 7.4 %convolution_convert_fusion = bf16[256,4,24,128]{3,0,2,1:T(8,128)(2,1)S(1)} fusion(bf16[4,24,384,128]{3,2,1,0:T(8,128)(2,1)} %param.9, f32[384,128]{0,1:T(8,128)S(1)} %get-tuple-element.3, f32[384,128]{0,1:T(8,128)S(1)} %get-tuple-element.4), kind=kOutput, calls=%fused_computation.19 | convolution fusion | flops 2419359744 | bytes 16121856 | tf_op jit(solution)/shard_map/blxc,xk->blkc/dot_general | solution.py:44
  26.3 1.1 fusion.22
  33.9 3.3 all-to-all-done.1
  37.2 4.7 all-to-all-start
  42.3 136.9 %all-to-all-done = bf16[8,4,24,2,16,128]{5,4,3,2,1,0:T(8,128)(2,1)} async-done(((bf16[8,4,24,2,16,128]{5,4,3,2,1,0:T(8,128)(2,1)}), bf16[8,4,24,2,16,128]{5,4,3,2,1,0:T(8,128)(2,1)}, u32[]{:S(2)}, u32[]{:S(2)}) %all-to-all-start) | async-done | bytes 6291488 | tf_op jit(solution)/shard_map/all_to_all | solution.py:10
  179.2 7.2 %copy.25 = bf16[8,4,24,2,16,128]{5,4,3,2,0,1:T(8,128)(2,1)} copy(bf16[8,4,24,2,16,128]{5,4,3,2,1,0:T(8,128)(2,1)} %all-to-all-done) | data formatting | bytes 12582912 | tf_op jit(solution)/shard_map/all_to_all | solution.py:10
  186.4 8.4 %convert_bitcast_fusion = bf16[4,192,2,16,128]{4,1,2,0,3:T(8,128)(2,1)} fusion(bf16[192,16,128,1,1]{2,0,4,3,1:T(8,128)(2,1)S(1)} %bitcast.98, f32[128,128]{0,1:T(8,128)S(1)} %add_divide_fusion, f32[16,128]{1,0:T(8,128)S(1)} %fusion.35, bf16[4,192,2,16,128]{4,3,2,1,0:T(8,128)(2,1)} %bitcast.96), kind=kOutput, calls=%fused_computation.13 | convolution fusion | flops 1620049920 | bytes 13443072 | tf_op jit(solution)/shard_map/lmn,brmnc->blrmc/dot_general | solution.py:61
  194.8 9.5 %copy.30 = bf16[4,192,2,16,128]{4,2,0,3,1:T(2,128)(2,1)S(1)} copy(bf16[4,192,2,16,128]{4,1,2,0,3:T(8,128)(2,1)} %convert_bitcast_fusion) | data formatting | bytes 12582912 | tf_op jit(solution)/shard_map/convert_element_type | solution.py:63
  204.3 141.6 %all_to_all.38 = bf16[4,192,2,16,128]{4,2,0,3,1:T(2,128)(2,1)S(1)} all-to-all(bf16[4,192,2,16,128]{4,2,0,3,1:T(2,128)(2,1)S(1)} %copy.30), channel_id=1, replica_groups=mesh['grp'=4,'lat'=8] {'lat'}, dimensions={1} | all-to-all | bytes 12582912 | tf_op jit(solution)/shard_map/all_to_all | solution.py:64
  345.9 1.8 copy.31
  347.8 2.7 fusion.33
  350.4 6.4 %copy-done.2 = f32[384,4,24,128]{3,0,2,1:T(8,128)} copy-done((f32[384,4,24,128]{3,0,2,1:T(8,128)}, f32[384,4,24,128]{3,0,2,1:T(8,128)S(1)}, u32[]{:S(2)}) %copy-start.2) | copy-done | bytes 18874392
  356.9 4.3 bitcast_convert_fusion
  361.2 17.0 %fusion.44 = f32[36864,256]{1,0:T(8,128)} fusion(bf16[36864,128]{1,0:T(8,128)(2,1)} %bitcast_convert_fusion, bf16[128,256]{1,0:T(8,128)(2,1)S(1)} %copy-done.3), kind=kOutput, calls=%fused_computation.62 | convolution fusion | flops 2415919104 | bytes 47251456 | tf_op jit(solution)/shard_map/dot_general | solution.py:71
  378.1 27.9 %fusion.2 = f32[36864,256]{1,0:T(8,128)} fusion(bf16[256,256]{1,0:T(8,128)(2,1)S(1)} %copy-done, f32[36864,256]{1,0:T(8,128)} %fusion.44, bf16[36864,128]{1,0:T(8,128)(2,1)} %bitcast.99, bf16[128,256]{1,0:T(8,128)(2,1)S(1)} %copy-done.5, f32[256]{0:T(256)S(1)} %copy-done.7), kind=kOutput, calls=%fused_computation.8 | convolution fusion | flops 7313817600 | bytes 85132288 | tf_op jit(solution)/shard_map/dot_general | solution.py:79
  406.0 24.7 %fusion.1 = bf16[36864,128]{1,0:T(8,128)(2,1)} fusion(f32[36864,128]{1,0:T(8,128)} %bitcast.82, bf16[256,128]{1,0:T(8,128)(2,1)S(1)} %copy-done.6, f32[36864,256]{1,0:T(8,128)} %fusion.2), kind=kOutput, calls=%fused_computation.3 | convolution fusion | flops 2472542208 | bytes 66125824 | tf_op jit(solution)/shard_map/dot_general | solution.py:81
  430.7 7.6 %reduce_sum.21 = bf16[24,384,128]{2,1,0:T(8,128)(2,1)} reduce(bf16[4,24,384,128]{3,2,1,0:T(8,128)(2,1)} %bitcast.91, bf16[]{:T(256)} %constant.37.clone.1), dimensions={0}, to_apply=%region_0.1 | reduce | flops 3538944 | bytes 11796482 | tf_op jit(solution)/shard_map/reduce_sum | solution.py:85
  438.3 54.8 %all-reduce.3.cloned.1.call-done = bf16[24,384,128]{2,1,0:T(8,128)(2,1)} async-done(((bf16[24,384,128]{2,1,0:T(8,128)(2,1)}), bf16[24,384,128]{2,1,0:T(8,128)(2,1)}) %all-reduce.3.cloned.1.call-update) | async-done | bytes 2359312 | tf_op jit(solution)/shard_map/psum | solution.py:85
  493.1 4.4 convert_multiply_fusion.1
  497.5 9.8 %multiply_reduce_fusion = bf16[24,384,128]{2,1,0:T(8,128)(2,1)} fusion(bf16[4,24,384,128]{3,2,1,0:T(8,128)(2,1)} %bitcast.92, f32[24,384,128]{2,1,0:T(8,128)} %convert_multiply_fusion.1), kind=kLoop, calls=%fused_computation.7 | loop fusion | flops 17694720 | bytes 16515072 | tf_op jit(solution)/shard_map/reduce_sum | solution.py:90
  507.3 55.9 %all-reduce.5.cloned.1.call-done = bf16[24,384,128]{2,1,0:T(8,128)(2,1)} async-done(((bf16[24,384,128]{2,1,0:T(8,128)(2,1)}), bf16[24,384,128]{2,1,0:T(8,128)(2,1)}) %all-reduce.5.cloned.1.call-update) | async-done | bytes 2359312 | tf_op jit(solution)/shard_map/psum | solution.py:89
  563.2 4.4 convert_multiply_fusion
  (32 shorter events, 8.8 us)
Async XLA Ops:
  7.2 371.0 %copy-start = (bf16[256,256]{1,0:T(8,128)(2,1)S(1)}, bf16[256,256]{1,0:T(8,128)(2,1)}, u32[]{:S(2)}) copy-start(bf16[256,256]{1,0:T(8,128)(2,1)} %param.16) | copy-start | bytes 393220
  9.7 27.5 %all-to-all-start.1 = ((bf16[24,128,128]{2,0,1:T(8,128)(2,1)}), bf16[24,128,128]{2,0,1:T(8,128)(2,1)S(1)}, u32[]{:S(2)}, u32[]{:S(2)}) async-start(bf16[24,128,128]{2,0,1:T(8,128)(2,1)} %copy.26), calls=%async_computation.1 | async-start | bytes 1572864 | tf_op jit(solution)/shard_map/all_to_all | solution.py:48
  33.9 8.2 %copy-start.4 = (f32[128]{0:T(128)S(1)}, f32[128]{0:T(128)}, u32[]{:S(2)}) copy-start(f32[128]{0:T(128)} %param.12) | copy-start | bytes 1540
  37.2 142.0 %all-to-all-start = ((bf16[8,4,24,2,16,128]{5,4,3,2,1,0:T(8,128)(2,1)}), bf16[8,4,24,2,16,128]{5,4,3,2,1,0:T(8,128)(2,1)}, u32[]{:S(2)}, u32[]{:S(2)}) async-start(bf16[8,4,24,2,16,128]{5,4,3,2,1,0:T(8,128)(2,1)} %fusion.16), calls=%async_computation | async-start | bytes 12582912 | tf_op jit(solution)/shard_map/all_to_all | solution.py:10
  42.0 451.2 %all-reduce.3.cloned.1.call-start = ((), (), s32[]{:S(2)}) async-start(), calls=%async_computation.3 | async-start | bytes 4718592 | tf_op jit(solution)/shard_map/psum | solution.py:85
  350.4 6.5 %copy-start.2 = (f32[384,4,24,128]{3,0,2,1:T(8,128)}, f32[384,4,24,128]{3,0,2,1:T(8,128)S(1)}, u32[]{:S(2)}) copy-start(f32[384,4,24,128]{3,0,2,1:T(8,128)S(1)} %fusion.33) | copy-start | bytes 56623108
  356.9 4.3 copy-start.3
  361.2 17.0 %copy-start.5 = (bf16[128,256]{1,0:T(8,128)(2,1)S(1)}, bf16[128,256]{1,0:T(8,128)(2,1)}, u32[]{:S(2)}) copy-start(bf16[128,256]{1,0:T(8,128)(2,1)} %param.14) | copy-start | bytes 196612
  361.2 17.0 %copy-start.7 = (f32[256]{0:T(256)S(1)}, f32[256]{0:T(256)}, u32[]{:S(2)}) copy-start(f32[256]{0:T(256)} %param.15) | copy-start | bytes 3076
  378.1 27.9 %copy-start.6 = (bf16[256,128]{1,0:T(8,128)(2,1)S(1)}, bf16[256,128]{1,0:T(8,128)(2,1)}, u32[]{:S(2)}) copy-start(bf16[256,128]{1,0:T(8,128)(2,1)} %param.17) | copy-start | bytes 196612
  438.3 124.9 %all-reduce.5.cloned.1.call-start = ((), (), s32[]{:S(2)}) async-start(), calls=%async_computation.4 | async-start | bytes 4718592 | tf_op jit(solution)/shard_map/psum | solution.py:89
  497.5 70.1 %copy-start.1 = (bf16[256,256]{1,0:T(8,128)(2,1)S(1)}, bf16[256,256]{1,0:T(8,128)(2,1)}, u32[]{:S(2)}) copy-start(bf16[256,256]{1,0:T(8,128)(2,1)} %param.16) | copy-start | bytes 393220
Sparse Core Ops, SparseCore 0:
  438.4 54.6 all-reduce.2
  507.4 55.7 all-reduce.4
